TPU v7x, 32 devices: a whole 2x2x4 slice. The times are simulated.
32 devices in a mesh: kpt: 4 (over y, x), pw: 8 (over z, core).
Axes of the slice: x: 2, y: 2, z: 4, core: 2. Of those that a mesh axis runs over, the one named last changes fastest.
Arguments:
- energies: float32 [16, 512], P('kpt', 'pw'), may hold values from 0.5 to 3
- current: float32 [2, 16, 512], P(None, 'kpt', 'pw'), may hold values from -40 to 40
- previous: float32 [2, 16, 512], P(None, 'kpt', 'pw'), may hold values from -6 to 6
- previous_beta: float32 [2], replicated, may hold values from 0.5 to 2
- pair_left: bfloat16 [16, 512, 4096], P('kpt', None, 'pw'), may hold values from -0.09375 to 0.09375
- pair_right: bfloat16 [16, 512, 4096], P('kpt', None, 'pw'), may hold values from -0.25 to 0.25
- screened: bfloat16 [16, 4096, 4096], P('kpt', 'pw'), may hold values from -0.0234375 to 0.0234375
- momentum_index: int32 [16, 16], replicated, may hold values from 0 to 15, each once within a row
Outputs:
- last_vector: float32 [2, 16, 512], P(None, 'kpt', 'pw')
- prior_vector: float32 [2, 16, 512], P(None, 'kpt', 'pw')
- alpha_terms: float32 [2, 3], replicated
- beta_terms: float32 [2, 3], replicated
Inputs may be any that keep to these rules, and one draw needn't show every extreme that they name: Each row of momentum_index names every index from 0 to 15 once.
All inputs are finite; a program needn't handle non-finite values.
Results may differ from a plain program's by a relative error of at most 0.003.
Values may be sent and summed in bfloat16 or wider, within the bound.
A program may use at most 128 MiB of HBM per device.

v0:
```python
import jax
import jax.numpy as jnp
from jax import lax
from jax.sharding import PartitionSpec as P

STEPS = 3
epsilon = 1e-06


def screened_images(density, screened):
    kpoint_rows = lax.all_gather(density, "kpt", axis=0, tiled=True)
    return jnp.einsum(
        "qsg,kvg->qkvs",
        screened,
        lax.all_gather(kpoint_rows, "pw", axis=2, tiled=True),
        preferred_element_type=jnp.float32,
    )


def on_device(
    energies, current, previous, previous_beta, pair_left, pair_right, screened, momentum_index
):
    kpoint_total = momentum_index.shape[0]
    band_total = pair_left.shape[1]
    entries = kpoint_total * band_total
    qcount = screened.shape[0]
    qpoints = lax.axis_index("kpt") * qcount + jnp.arange(qcount, dtype=jnp.int32)
    selector = (momentum_index[None, :, :] == qpoints[:, None, None]).astype(jnp.float32)
    vector, earlier, levels = (current, previous, energies)
    beta_before = previous_beta
    alpha_list = []
    beta_list = []
    for turn_index in range(STEPS):
        rounded = vector.astype(jnp.bfloat16)
        rounded = lax.all_gather(rounded, "pw", axis=2, tiled=True)
        density = jnp.einsum(
            "kcg,vkc->kvg", pair_right, rounded, preferred_element_type=jnp.float32
        ).astype(jnp.bfloat16)
        images = screened_images(density, screened)
        partial_field = jnp.einsum(
            "qjk,qkvs->jvs",
            selector,
            images,
            precision=lax.Precision.HIGHEST,
            preferred_element_type=jnp.float32,
        )
        potential = lax.psum_scatter(partial_field, "kpt", scatter_dimension=0, tiled=True).astype(
            jnp.bfloat16
        )
        partial_direct = jnp.einsum(
            "kcs,kvs->vkc", pair_left, potential, preferred_element_type=jnp.float32
        )
        direct = lax.psum_scatter(partial_direct, "pw", scatter_dimension=2, tiled=True)
        applied = levels[None] * vector - direct - beta_before[:, None, None] * earlier
        vector_own = vector
        cross_sum, square_sum, vector_sum = lax.psum(
            (
                jnp.sum(vector_own * applied, axis=(1, 2)),
                jnp.sum(applied * applied, axis=(1, 2)),
                jnp.sum(vector_own * vector_own, axis=(1, 2)),
            ),
            ("kpt", "pw"),
        )
        alpha_now = cross_sum / entries
        mean_square = (
            square_sum / entries
            - 2.0 * alpha_now * (cross_sum / entries)
            + alpha_now * alpha_now * (vector_sum / entries)
        )
        beta_now = jnp.sqrt(mean_square + epsilon)
        residual = applied - alpha_now[:, None, None] * vector
        earlier = vector
        vector = residual / beta_now[:, None, None]
        beta_before = beta_now
        alpha_list.append(alpha_now)
        beta_list.append(beta_now)
    return (vector, earlier, jnp.stack(alpha_list, axis=1), jnp.stack(beta_list, axis=1))


def solution(mesh):
    return jax.shard_map(
        on_device,
        mesh=mesh,
        in_specs=(
            P("kpt", "pw"),
            P(None, "kpt", "pw"),
            P(None, "kpt", "pw"),
            P(),
            P("kpt", None, "pw"),
            P("kpt", None, "pw"),
            P("kpt", "pw", None),
            P(),
        ),
        out_specs=(P(None, "kpt", "pw"), P(None, "kpt", "pw"), P(), P()),
        check_vma=False,
    )
```

profile of v0, /device:TPU:10, one launch (start us, length us, event | category | flops | bytes accessed | tf_op | source)
XLA Modules:
  0.0 434.7 jit_solution(2461469843560152316)
XLA Ops:
  8.2 14.4 %all_gather.27 = bf16[2,4,512]{1,0,2:T(2,128)(2,1)S(1)} all-gather(bf16[2,4,64]{1,0,2:T(2,128)(2,1)S(1)} %copy.33), channel_id=1, replica_groups=mesh['kpt'=4,'pw'=8] {'pw'}, dimensions={2}, use_global_device_ids=true | all-gather | bytes 9216 | tf_op jit(solution)/shard_map/all_gather | solution.py:35
  23.2 8.2 %all_gather.28 = bf16[16,2,512]{2,1,0:T(2,128)(2,1)S(1)} all-gather(bf16[4,2,512]{2,1,0:T(2,128)(2,1)S(1)} %convolution_convert_fusion.2), channel_id=1, replica_groups=mesh['kpt'=4,'pw'=8] {'kpt'}, dimensions={0}, use_global_device_ids=true | all-gather | bytes 40960 | tf_op jit(solution)/shard_map/all_gather | solution.py:11
  31.4 14.3 %all_gather.29 = bf16[16,2,4096]{2,0,1:T(8,128)(2,1)S(1)} all-gather(bf16[16,2,512]{2,0,1:T(8,128)(2,1)S(1)} %copy.35), channel_id=1, replica_groups=mesh['kpt'=4,'pw'=8] {'pw'}, dimensions={2}, use_global_device_ids=true | all-gather | bytes 294912 | tf_op jit(solution)/shard_map/all_gather | solution.py:15
  45.6 10.8 %fusion.6 = f32[4,16,2,512]{3,1,0,2:T(8,128)S(1)} fusion(bf16[4,512,4096]{2,1,0:T(8,128)(2,1)} %param.14, bf16[16,2,4096]{2,0,1:T(8,128)(2,1)S(1)} %all_gather.29), kind=kOutput, calls=%fused_computation.6 | convolution fusion | flops 536870912 | bytes 17301504 | tf_op jit(solution)/shard_map/qsg,kvg->qkvs/dot_general | solution.py:12
  56.9 15.0 %all-reduce = bf16[16,2,512]{2,1,0:T(2,128)(2,1)S(1)} all-reduce(f32[16,2,512]{2,1,0:T(2,128)S(1)} %copy.36), channel_id=2, replica_groups=mesh['kpt'=4,'pw'=8] {'kpt'}, use_global_device_ids=true, to_apply=%region_0.0.clone | all-reduce | flops 16384 | bytes 98304
  73.2 2.2 convolution_bitcast_fusion.5
  77.1 28.3 %reduce-scatter.10.cloned.1.call-done = f32[64,8]{1,0:T(8,128)} async-done(((f32[512,8]{1,0:T(8,128)}), f32[64,8]{1,0:T(8,128)}) %reduce-scatter.10.cloned.1.call-update) | async-done | bytes 2064
  106.6 43.5 %all-reduce.5 = (f32[2]{0:T(128)S(1)}, f32[2]{0:T(128)S(1)}, f32[2]{0:T(128)S(1)}) all-reduce(f32[2]{0:T(128)S(1)} %get-tuple-element.24, f32[2]{0:T(128)S(1)} %get-tuple-element.23, f32[2]{0:T(128)S(1)} %get-tuple-element.22), channel_id=1, replica_groups=mesh['kpt'=4,'pw'=8] {'kpt','pw'}, use_global_device_ids=true, to_apply=%region_7.0 | all-reduce | flops 6 | bytes 48 | tf_op jit(solution)/shard_map/psum | solution.py:56
  150.4 12.4 %all_gather.30 = bf16[2,4,512]{1,0,2:T(2,128)(2,1)S(1)} all-gather(bf16[2,4,64]{1,0,2:T(2,128)(2,1)S(1)} %copy.38), channel_id=1, replica_groups=mesh['kpt'=4,'pw'=8] {'pw'}, dimensions={2}, use_global_device_ids=true | all-gather | bytes 9216 | tf_op jit(solution)/shard_map/all_gather | solution.py:35
  163.3 7.2 %all_gather.31 = bf16[16,2,512]{2,1,0:T(2,128)(2,1)S(1)} all-gather(bf16[4,2,512]{2,1,0:T(2,128)(2,1)S(1)} %convolution_convert_fusion.1), channel_id=1, replica_groups=mesh['kpt'=4,'pw'=8] {'kpt'}, dimensions={0}, use_global_device_ids=true | all-gather | bytes 40960 | tf_op jit(solution)/shard_map/all_gather | solution.py:11
  170.5 14.4 %all_gather.32 = bf16[16,2,4096]{2,0,1:T(8,128)(2,1)S(1)} all-gather(bf16[16,2,512]{2,0,1:T(8,128)(2,1)S(1)} %copy.40), channel_id=1, replica_groups=mesh['kpt'=4,'pw'=8] {'pw'}, dimensions={2}, use_global_device_ids=true | all-gather | bytes 294912 | tf_op jit(solution)/shard_map/all_gather | solution.py:15
  184.9 10.8 %fusion.9 = f32[4,16,2,512]{3,1,0,2:T(8,128)S(1)} fusion(bf16[4,512,4096]{2,1,0:T(8,128)(2,1)} %param.14, bf16[16,2,4096]{2,0,1:T(8,128)(2,1)S(1)} %all_gather.32), kind=kOutput, calls=%fused_computation.7 | convolution fusion | flops 536870912 | bytes 17301504 | tf_op jit(solution)/shard_map/qsg,kvg->qkvs/dot_general | solution.py:12
  196.2 15.7 %all-reduce.1 = bf16[16,2,512]{2,1,0:T(2,128)(2,1)S(1)} all-reduce(f32[16,2,512]{2,1,0:T(2,128)S(1)} %copy.41), channel_id=4, replica_groups=mesh['kpt'=4,'pw'=8] {'kpt'}, use_global_device_ids=true, to_apply=%region_8.0.clone | all-reduce | flops 16384 | bytes 98304
  211.8 2.2 convolution_bitcast_fusion.4
  215.8 27.7 %reduce-scatter.12.cloned.1.call-done = f32[64,8]{1,0:T(8,128)} async-done(((f32[512,8]{1,0:T(8,128)}), f32[64,8]{1,0:T(8,128)}) %reduce-scatter.12.cloned.1.call-update) | async-done | bytes 2064
  244.7 43.5 %all-reduce.4 = (f32[2]{0:T(128)S(1)}, f32[2]{0:T(128)S(1)}, f32[2]{0:T(128)S(1)}) all-reduce(f32[2]{0:T(128)S(1)} %get-tuple-element.21, f32[2]{0:T(128)S(1)} %get-tuple-element.20, f32[2]{0:T(128)S(1)} %get-tuple-element.19), channel_id=1, replica_groups=mesh['kpt'=4,'pw'=8] {'kpt','pw'}, use_global_device_ids=true, to_apply=%region_15.0 | all-reduce | flops 6 | bytes 48 | tf_op jit(solution)/shard_map/psum | solution.py:56
  288.3 12.4 %all_gather.33 = bf16[2,4,512]{1,0,2:T(2,128)(2,1)S(1)} all-gather(bf16[2,4,64]{1,0,2:T(2,128)(2,1)S(1)} %copy.43), channel_id=1, replica_groups=mesh['kpt'=4,'pw'=8] {'pw'}, dimensions={2}, use_global_device_ids=true | all-gather | bytes 9216 | tf_op jit(solution)/shard_map/all_gather | solution.py:35
  301.3 7.3 %all_gather.34 = bf16[16,2,512]{2,1,0:T(2,128)(2,1)S(1)} all-gather(bf16[4,2,512]{2,1,0:T(2,128)(2,1)S(1)} %convolution_convert_fusion), channel_id=1, replica_groups=mesh['kpt'=4,'pw'=8] {'kpt'}, dimensions={0}, use_global_device_ids=true | all-gather | bytes 40960 | tf_op jit(solution)/shard_map/all_gather | solution.py:11
  308.6 14.2 %all_gather.35 = bf16[16,2,4096]{2,0,1:T(8,128)(2,1)S(1)} all-gather(bf16[16,2,512]{2,0,1:T(8,128)(2,1)S(1)} %copy.45), channel_id=1, replica_groups=mesh['kpt'=4,'pw'=8] {'pw'}, dimensions={2}, use_global_device_ids=true | all-gather | bytes 294912 | tf_op jit(solution)/shard_map/all_gather | solution.py:15
  322.8 10.8 %fusion.12 = f32[4,16,2,512]{3,1,0,2:T(8,128)S(1)} fusion(bf16[4,512,4096]{2,1,0:T(8,128)(2,1)} %param.14, bf16[16,2,4096]{2,0,1:T(8,128)(2,1)S(1)} %all_gather.35), kind=kOutput, calls=%fused_computation.8 | convolution fusion | flops 536870912 | bytes 17301504 | tf_op jit(solution)/shard_map/qsg,kvg->qkvs/dot_general | solution.py:12
  334.1 15.6 %all-reduce.2 = bf16[16,2,512]{2,1,0:T(2,128)(2,1)S(1)} all-reduce(f32[16,2,512]{2,1,0:T(2,128)S(1)} %copy.46), channel_id=6, replica_groups=mesh['kpt'=4,'pw'=8] {'kpt'}, use_global_device_ids=true, to_apply=%region_16.0.clone | all-reduce | flops 16384 | bytes 98304
  349.6 2.2 convolution_bitcast_fusion.3
  353.5 28.0 %reduce-scatter.14.cloned.1.call-done = f32[64,8]{1,0:T(8,128)} async-done(((f32[512,8]{1,0:T(8,128)}), f32[64,8]{1,0:T(8,128)}) %reduce-scatter.14.cloned.1.call-update) | async-done | bytes 2064
  382.7 43.5 %all-reduce.3 = (f32[2]{0:T(128)S(1)}, f32[2]{0:T(128)S(1)}, f32[2]{0:T(128)S(1)}) all-reduce(f32[2]{0:T(128)S(1)} %get-tuple-element.18, f32[2]{0:T(128)S(1)} %get-tuple-element.17, f32[2]{0:T(128)S(1)} %get-tuple-element.16), channel_id=1, replica_groups=mesh['kpt'=4,'pw'=8] {'kpt','pw'}, use_global_device_ids=true, to_apply=%region_23.0 | all-reduce | flops 6 | bytes 48 | tf_op jit(solution)/shard_map/psum | solution.py:56
  (68 shorter events, 15.3 us)
Async XLA Ops:
  7.2 15.6 %copy-start = (bf16[4,512,512]{2,1,0:T(8,128)(2,1)S(1)}, bf16[4,512,512]{2,1,0:T(8,128)(2,1)}, u32[]{:S(2)}) copy-start(bf16[4,512,512]{2,1,0:T(8,128)(2,1)} %param.13) | copy-start | bytes 6291460
  7.2 98.2 %reduce-scatter.10.cloned.1.call-start = ((), (), s32[]{:S(2)}) async-start(), calls=%async_computation.3 | async-start | bytes 294912
  45.6 10.8 %copy-start.1 = (s32[16,16]{1,0:T(8,128)S(1)}, s32[16,16]{1,0:T(8,128)}, u32[]{:S(2)}) copy-start(s32[16,16]{1,0:T(8,128)} %param.15) | copy-start | bytes 3076
  45.6 26.3 %copy-start.7 = (u32[32]{0:T(128)S(1)}, u32[32]{0:T(128)}, u32[]{:S(2)}) copy-start(u32[32]{0:T(128)} %constant.29) | copy-start | bytes 388
  73.2 33.2 %copy-start.2 = (f32[2,4,64]{2,1,0:T(4,128)S(1)}, f32[2,4,64]{2,1,0:T(4,128)}, u32[]{:S(2)}) copy-start(f32[2,4,64]{2,1,0:T(4,128)} %param.9) | copy-start | bytes 6148
  73.2 33.2 %copy-start.4 = (f32[4,64]{1,0:T(4,128)S(1)}, f32[4,64]{1,0:T(4,128)}, u32[]{:S(2)}) copy-start(f32[4,64]{1,0:T(4,128)} %param.8) | copy-start | bytes 3076
  73.2 33.2 %copy-start.5 = (f32[2,4,64]{2,1,0:T(4,128)S(1)}, f32[2,4,64]{2,1,0:T(4,128)}, u32[]{:S(2)}) copy-start(f32[2,4,64]{2,1,0:T(4,128)} %param.10) | copy-start | bytes 6148
  73.2 33.2 %copy-start.6 = (f32[2]{0:T(128)S(1)}, f32[2]{0:T(128)}, u32[]{:S(2)}) copy-start(f32[2]{0:T(128)} %param.11) | copy-start | bytes 28
  77.1 166.4 %reduce-scatter.12.cloned.1.call-start = ((), (), s32[]{:S(2)}) async-start(), calls=%async_computation.4 | async-start | bytes 294912
  215.7 165.8 %reduce-scatter.14.cloned.1.call-start = ((), (), s32[]{:S(2)}) async-start(), calls=%async_computation.5 | async-start | bytes 294912
  288.2 139.3 %copy-start.3 = (f32[2,4,64]{2,1,0:T(4,128)}, f32[2,4,64]{2,1,0:T(4,128)S(1)}, u32[]{:S(2)}) copy-start(f32[2,4,64]{2,1,0:T(4,128)S(1)} %get-tuple-element.36) | copy-start | bytes 6148
Sparse Core Ops, SparseCore 0:
  77.2 28.1 reduce-scatter.9
  215.8 27.6 reduce-scatter.11
  353.6 27.8 reduce-scatter.13
where the time goes:
time: 436 us; the launch traced here: 435 us
  blocking collectives  282 us (65%)
  waiting for transfers between devices  84.1 us (19%)
  matrix products  41.3 us (9%)
  between operations  14.7 us (3%)
  local copies, waits for them, and re-layouts  10.7 us (2%)
    psum x3, blocking collectives, on_device(): lax.psum((jnp.sum(vector_own * applied, axis=(1, 2)), jnp.sum(applied * a...  130 us
    unnamed x6, waiting for transfers between devices  84.1 us
    unnamed x3, blocking collectives  46.3 us
    all_gather x3, blocking collectives, screened_images(): lax.all_gather(kpoint_rows, 'pw', axis=2, tiled=True)  42.9 us
    all_gather x3, blocking collectives, on_device(): rounded = lax.all_gather(rounded, 'pw', axis=2, tiled=True)  39.2 us
    dot_general x3, matrix products, screened_images(): jnp.einsum('qsg,kvg->qkvs', screened, lax.all_gather(kpoint_rows, 'pw', a...  32.4 us
    all_gather x3, blocking collectives, screened_images(): kpoint_rows = lax.all_gather(density, 'kpt', axis=0, tiled=True)  22.8 us
    unnamed x28, local copies, waits for them, and re-layouts  9.34 us
  transfers between devices with their start and end apart: 3, of which 3 were waited for; matrix products, arithmetic and copies ran while one was open for 0% of the time, Pallas kernels for 0%

commit v1 on v0

--- a/solution.py
+++ b/solution.py
@@ -53,13 +53,17 @@
         direct = lax.psum_scatter(partial_direct, "pw", scatter_dimension=2, tiled=True)
         applied = levels[None] * vector - direct - beta_before[:, None, None] * earlier
         vector_own = vector
-        cross_sum, square_sum, vector_sum = lax.psum(
+
+        def expand_things_on_mesh(buf):
+            found_now = lax.psum(buf, "kpt")
+            return lax.psum(found_now, axis_name="pw")
+
+        cross_sum, square_sum, vector_sum = expand_things_on_mesh(
             (
                 jnp.sum(vector_own * applied, axis=(1, 2)),
                 jnp.sum(applied * applied, axis=(1, 2)),
                 jnp.sum(vector_own * vector_own, axis=(1, 2)),
-            ),
-            ("kpt", "pw"),
+            )
         )
         alpha_now = cross_sum / entries
         mean_square = (

time: 436 us -> 386 us (0.89)
  the two profiles are of different devices: /device:TPU:10 before, /device:TPU:0 now
where the time goes in v1:
time: 386 us; the launch traced here: 385 us
  blocking collectives  229 us (59%)
  waiting for transfers between devices  87.3 us (23%)
  matrix products  41.3 us (11%)
  between operations  14.7 us (4%)
  local copies, waits for them, and re-layouts  10.7 us (3%)
    unnamed x6, waiting for transfers between devices  87.3 us
    unnamed x3, blocking collectives  48.4 us
    all_gather x3, blocking collectives, on_device(): rounded = lax.all_gather(rounded, 'pw', axis=2, tiled=True)  44.3 us
    all_gather x3, blocking collectives, screened_images(): lax.all_gather(kpoint_rows, 'pw', axis=2, tiled=True)  43 us
    psum x3, blocking collectives, expand_things_on_mesh(): return lax.psum(found_now, axis_name='pw')  40.8 us
    dot_general x3, matrix products, screened_images(): jnp.einsum('qsg,kvg->qkvs', screened, lax.all_gather(kpoint_rows, 'pw', a...  32.4 us
    psum x3, blocking collectives, expand_things_on_mesh(): found_now = lax.psum(buf, 'kpt')  29.5 us
    all_gather x3, blocking collectives, screened_images(): kpoint_rows = lax.all_gather(density, 'kpt', axis=0, tiled=True)  22.7 us
  transfers between devices with their start and end apart: 3, of which 3 were waited for; matrix products, arithmetic and copies ran while one was open for 0% of the time, Pallas kernels for 0%

profile of v1, /device:TPU:0, one launch (start us, length us, event | category | flops | bytes accessed | tf_op | source)
XLA Modules:
  0.0 385.0 jit_solution(17494946835726596548)
XLA Ops:
  8.2 15.9 %all_gather.27 = bf16[2,4,512]{1,0,2:T(2,128)(2,1)S(1)} all-gather(bf16[2,4,64]{1,0,2:T(2,128)(2,1)S(1)} %copy.33), channel_id=1, replica_groups=mesh['kpt'=4,'pw'=8] {'pw'}, dimensions={2}, use_global_device_ids=true | all-gather | bytes 9216 | tf_op jit(solution)/shard_map/all_gather | solution.py:35
  24.7 8.2 %all_gather.28 = bf16[16,2,512]{2,1,0:T(2,128)(2,1)S(1)} all-gather(bf16[4,2,512]{2,1,0:T(2,128)(2,1)S(1)} %convolution_convert_fusion.2), channel_id=1, replica_groups=mesh['kpt'=4,'pw'=8] {'kpt'}, dimensions={0}, use_global_device_ids=true | all-gather | bytes 40960 | tf_op jit(solution)/shard_map/all_gather | solution.py:11
  32.9 14.3 %all_gather.29 = bf16[16,2,4096]{2,0,1:T(8,128)(2,1)S(1)} all-gather(bf16[16,2,512]{2,0,1:T(8,128)(2,1)S(1)} %copy.35), channel_id=1, replica_groups=mesh['kpt'=4,'pw'=8] {'pw'}, dimensions={2}, use_global_device_ids=true | all-gather | bytes 294912 | tf_op jit(solution)/shard_map/all_gather | solution.py:15
  47.2 10.8 %fusion.6 = f32[4,16,2,512]{3,1,0,2:T(8,128)S(1)} fusion(bf16[4,512,4096]{2,1,0:T(8,128)(2,1)} %param.14, bf16[16,2,4096]{2,0,1:T(8,128)(2,1)S(1)} %all_gather.29), kind=kOutput, calls=%fused_computation.6 | convolution fusion | flops 536870912 | bytes 17301504 | tf_op jit(solution)/shard_map/qsg,kvg->qkvs/dot_general | solution.py:12
  58.4 16.0 %all-reduce = bf16[16,2,512]{2,1,0:T(2,128)(2,1)S(1)} all-reduce(f32[16,2,512]{2,1,0:T(2,128)S(1)} %copy.36), channel_id=2, replica_groups=mesh['kpt'=4,'pw'=8] {'kpt'}, use_global_device_ids=true, to_apply=%region_0.0.clone | all-reduce | flops 16384 | bytes 98304
  79.7 31.0 %reduce-scatter.10.cloned.1.call-done = f32[64,8]{1,0:T(8,128)} async-done(((f32[512,8]{1,0:T(8,128)}), f32[64,8]{1,0:T(8,128)}) %reduce-scatter.10.cloned.1.call-update) | async-done | bytes 2064
  111.9 9.8 %all-reduce.8 = (f32[2]{0:T(128)S(1)}, f32[2]{0:T(128)S(1)}, f32[2]{0:T(128)S(1)}) all-reduce(f32[2]{0:T(128)S(1)} %get-tuple-element.24, f32[2]{0:T(128)S(1)} %get-tuple-element.23, f32[2]{0:T(128)S(1)} %get-tuple-element.22), channel_id=1, replica_groups=mesh['kpt'=4,'pw'=8] {'kpt'}, use_global_device_ids=true, to_apply=%region_9.0 | all-reduce | flops 6 | bytes 48 | tf_op jit(solution)/shard_map/psum | solution.py:58
  121.7 13.6 %all-reduce.5 = (f32[2]{0:T(128)S(1)}, f32[2]{0:T(128)S(1)}, f32[2]{0:T(128)S(1)}) all-reduce(f32[2]{0:T(128)S(1)} %get-tuple-element.40, f32[2]{0:T(128)S(1)} %get-tuple-element.41, f32[2]{0:T(128)S(1)} %get-tuple-element.42), channel_id=1, replica_groups=mesh['kpt'=4,'pw'=8] {'pw'}, use_global_device_ids=true, to_apply=%region_10.0 | all-reduce | flops 6 | bytes 48 | tf_op jit(solution)/shard_map/psum | solution.py:59
  135.6 14.2 %all_gather.30 = bf16[2,4,512]{1,0,2:T(2,128)(2,1)S(1)} all-gather(bf16[2,4,64]{1,0,2:T(2,128)(2,1)S(1)} %copy.38), channel_id=1, replica_groups=mesh['kpt'=4,'pw'=8] {'pw'}, dimensions={2}, use_global_device_ids=true | all-gather | bytes 9216 | tf_op jit(solution)/shard_map/all_gather | solution.py:35
  150.3 7.3 %all_gather.31 = bf16[16,2,512]{2,1,0:T(2,128)(2,1)S(1)} all-gather(bf16[4,2,512]{2,1,0:T(2,128)(2,1)S(1)} %convolution_convert_fusion.1), channel_id=1, replica_groups=mesh['kpt'=4,'pw'=8] {'kpt'}, dimensions={0}, use_global_device_ids=true | all-gather | bytes 40960 | tf_op jit(solution)/shard_map/all_gather | solution.py:11
  157.6 14.4 %all_gather.32 = bf16[16,2,4096]{2,0,1:T(8,128)(2,1)S(1)} all-gather(bf16[16,2,512]{2,0,1:T(8,128)(2,1)S(1)} %copy.40), channel_id=1, replica_groups=mesh['kpt'=4,'pw'=8] {'pw'}, dimensions={2}, use_global_device_ids=true | all-gather | bytes 294912 | tf_op jit(solution)/shard_map/all_gather | solution.py:15
  172.0 10.8 %fusion.9 = f32[4,16,2,512]{3,1,0,2:T(8,128)S(1)} fusion(bf16[4,512,4096]{2,1,0:T(8,128)(2,1)} %param.14, bf16[16,2,4096]{2,0,1:T(8,128)(2,1)S(1)} %all_gather.32), kind=kOutput, calls=%fused_computation.7 | convolution fusion | flops 536870912 | bytes 17301504 | tf_op jit(solution)/shard_map/qsg,kvg->qkvs/dot_general | solution.py:12
  183.2 16.2 %all-reduce.1 = bf16[16,2,512]{2,1,0:T(2,128)(2,1)S(1)} all-reduce(f32[16,2,512]{2,1,0:T(2,128)S(1)} %copy.41), channel_id=4, replica_groups=mesh['kpt'=4,'pw'=8] {'kpt'}, use_global_device_ids=true, to_apply=%region_11.0.clone | all-reduce | flops 16384 | bytes 98304
  203.3 28.1 %reduce-scatter.12.cloned.1.call-done = f32[64,8]{1,0:T(8,128)} async-done(((f32[512,8]{1,0:T(8,128)}), f32[64,8]{1,0:T(8,128)}) %reduce-scatter.12.cloned.1.call-update) | async-done | bytes 2064
  232.6 9.8 %all-reduce.7 = (f32[2]{0:T(128)S(1)}, f32[2]{0:T(128)S(1)}, f32[2]{0:T(128)S(1)}) all-reduce(f32[2]{0:T(128)S(1)} %get-tuple-element.21, f32[2]{0:T(128)S(1)} %get-tuple-element.20, f32[2]{0:T(128)S(1)} %get-tuple-element.19), channel_id=1, replica_groups=mesh['kpt'=4,'pw'=8] {'kpt'}, use_global_device_ids=true, to_apply=%region_20.0 | all-reduce | flops 6 | bytes 48 | tf_op jit(solution)/shard_map/psum | solution.py:58
  242.4 13.6 %all-reduce.4 = (f32[2]{0:T(128)S(1)}, f32[2]{0:T(128)S(1)}, f32[2]{0:T(128)S(1)}) all-reduce(f32[2]{0:T(128)S(1)} %get-tuple-element.37, f32[2]{0:T(128)S(1)} %get-tuple-element.38, f32[2]{0:T(128)S(1)} %get-tuple-element.39), channel_id=1, replica_groups=mesh['kpt'=4,'pw'=8] {'pw'}, use_global_device_ids=true, to_apply=%region_21.0 | all-reduce | flops 6 | bytes 48 | tf_op jit(solution)/shard_map/psum | solution.py:59
  256.2 14.2 %all_gather.33 = bf16[2,4,512]{1,0,2:T(2,128)(2,1)S(1)} all-gather(bf16[2,4,64]{1,0,2:T(2,128)(2,1)S(1)} %copy.43), channel_id=1, replica_groups=mesh['kpt'=4,'pw'=8] {'pw'}, dimensions={2}, use_global_device_ids=true | all-gather | bytes 9216 | tf_op jit(solution)/shard_map/all_gather | solution.py:35
  271.0 7.3 %all_gather.34 = bf16[16,2,512]{2,1,0:T(2,128)(2,1)S(1)} all-gather(bf16[4,2,512]{2,1,0:T(2,128)(2,1)S(1)} %convolution_convert_fusion), channel_id=1, replica_groups=mesh['kpt'=4,'pw'=8] {'kpt'}, dimensions={0}, use_global_device_ids=true | all-gather | bytes 40960 | tf_op jit(solution)/shard_map/all_gather | solution.py:11
  278.3 14.2 %all_gather.35 = bf16[16,2,4096]{2,0,1:T(8,128)(2,1)S(1)} all-gather(bf16[16,2,512]{2,0,1:T(8,128)(2,1)S(1)} %copy.45), channel_id=1, replica_groups=mesh['kpt'=4,'pw'=8] {'pw'}, dimensions={2}, use_global_device_ids=true | all-gather | bytes 294912 | tf_op jit(solution)/shard_map/all_gather | solution.py:15
  292.5 10.8 %fusion.12 = f32[4,16,2,512]{3,1,0,2:T(8,128)S(1)} fusion(bf16[4,512,4096]{2,1,0:T(8,128)(2,1)} %param.14, bf16[16,2,4096]{2,0,1:T(8,128)(2,1)S(1)} %all_gather.35), kind=kOutput, calls=%fused_computation.8 | convolution fusion | flops 536870912 | bytes 17301504 | tf_op jit(solution)/shard_map/qsg,kvg->qkvs/dot_general | solution.py:12
  303.7 16.2 %all-reduce.2 = bf16[16,2,512]{2,1,0:T(2,128)(2,1)S(1)} all-reduce(f32[16,2,512]{2,1,0:T(2,128)S(1)} %copy.46), channel_id=6, replica_groups=mesh['kpt'=4,'pw'=8] {'kpt'}, use_global_device_ids=true, to_apply=%region_22.0.clone | all-reduce | flops 16384 | bytes 98304
  323.7 28.1 %reduce-scatter.14.cloned.1.call-done = f32[64,8]{1,0:T(8,128)} async-done(((f32[512,8]{1,0:T(8,128)}), f32[64,8]{1,0:T(8,128)}) %reduce-scatter.14.cloned.1.call-update) | async-done | bytes 2064
  353.0 9.9 %all-reduce.6 = (f32[2]{0:T(128)S(1)}, f32[2]{0:T(128)S(1)}, f32[2]{0:T(128)S(1)}) all-reduce(f32[2]{0:T(128)S(1)} %get-tuple-element.18, f32[2]{0:T(128)S(1)} %get-tuple-element.17, f32[2]{0:T(128)S(1)} %get-tuple-element.16), channel_id=1, replica_groups=mesh['kpt'=4,'pw'=8] {'kpt'}, use_global_device_ids=true, to_apply=%region_31.0 | all-reduce | flops 6 | bytes 48 | tf_op jit(solution)/shard_map/psum | solution.py:58
  362.9 13.6 %all-reduce.3 = (f32[2]{0:T(128)S(1)}, f32[2]{0:T(128)S(1)}, f32[2]{0:T(128)S(1)}) all-reduce(f32[2]{0:T(128)S(1)} %get-tuple-element.34, f32[2]{0:T(128)S(1)} %get-tuple-element.35, f32[2]{0:T(128)S(1)} %get-tuple-element.36), channel_id=1, replica_groups=mesh['kpt'=4,'pw'=8] {'pw'}, use_global_device_ids=true, to_apply=%region_32.0 | all-reduce | flops 6 | bytes 48 | tf_op jit(solution)/shard_map/psum | solution.py:59
  (71 shorter events, 22.0 us)
Async XLA Ops:
  7.2 17.1 %copy-start = (bf16[4,512,512]{2,1,0:T(8,128)(2,1)S(1)}, bf16[4,512,512]{2,1,0:T(8,128)(2,1)}, u32[]{:S(2)}) copy-start(bf16[4,512,512]{2,1,0:T(8,128)(2,1)} %param.13) | copy-start | bytes 6291460
  7.2 103.6 %reduce-scatter.10.cloned.1.call-start = ((), (), s32[]{:S(2)}) async-start(), calls=%async_computation.3 | async-start | bytes 294912
  47.2 10.8 %copy-start.1 = (s32[16,16]{1,0:T(8,128)S(1)}, s32[16,16]{1,0:T(8,128)}, u32[]{:S(2)}) copy-start(s32[16,16]{1,0:T(8,128)} %param.15) | copy-start | bytes 3076
  47.2 27.3 %copy-start.7 = (u32[32]{0:T(128)S(1)}, u32[32]{0:T(128)}, u32[]{:S(2)}) copy-start(u32[32]{0:T(128)} %constant.29) | copy-start | bytes 388
  75.7 36.0 %copy-start.2 = (f32[2,4,64]{2,1,0:T(4,128)S(1)}, f32[2,4,64]{2,1,0:T(4,128)}, u32[]{:S(2)}) copy-start(f32[2,4,64]{2,1,0:T(4,128)} %param.9) | copy-start | bytes 6148
  75.7 36.0 %copy-start.4 = (f32[4,64]{1,0:T(4,128)S(1)}, f32[4,64]{1,0:T(4,128)}, u32[]{:S(2)}) copy-start(f32[4,64]{1,0:T(4,128)} %param.8) | copy-start | bytes 3076
  75.8 36.0 %copy-start.5 = (f32[2,4,64]{2,1,0:T(4,128)S(1)}, f32[2,4,64]{2,1,0:T(4,128)}, u32[]{:S(2)}) copy-start(f32[2,4,64]{2,1,0:T(4,128)} %param.10) | copy-start | bytes 6148
  75.8 36.0 %copy-start.6 = (f32[2]{0:T(128)S(1)}, f32[2]{0:T(128)}, u32[]{:S(2)}) copy-start(f32[2]{0:T(128)} %param.11) | copy-start | bytes 28
  79.6 151.8 %reduce-scatter.12.cloned.1.call-start = ((), (), s32[]{:S(2)}) async-start(), calls=%async_computation.4 | async-start | bytes 294912
  203.3 148.6 %reduce-scatter.14.cloned.1.call-start = ((), (), s32[]{:S(2)}) async-start(), calls=%async_computation.5 | async-start | bytes 294912
  256.1 121.7 %copy-start.3 = (f32[2,4,64]{2,1,0:T(4,128)}, f32[2,4,64]{2,1,0:T(4,128)S(1)}, u32[]{:S(2)}) copy-start(f32[2,4,64]{2,1,0:T(4,128)S(1)} %get-tuple-element.45) | copy-start | bytes 6148
Sparse Core Ops, SparseCore 0:
  79.8 30.9 reduce-scatter.9
  203.4 28.0 reduce-scatter.11
  323.9 27.9 reduce-scatter.13
